TPU v7x, 512 devices: a whole 4x8x8 slice. The times are simulated.
512 devices in a mesh: row: 32 (over y, x), col: 16 (over z, core).
Axes of the slice: x: 4, y: 8, z: 8, core: 2. Of those that a mesh axis runs over, the one named last changes fastest.
Arguments:
- state: float32 [8192, 16, 1024], P('row', 'col'), may hold values from -6 to 6
- coupling: bfloat16 [8192, 16, 1024], P('row', 'col'), may hold values from -2 to 2, as said below
- coupling_t: bfloat16 [2, 8192, 16, 1024], P(None, 'row', 'col'), may hold values from -2 to 2, as said below
- factor: float32 [4, 16, 256, 256], P(None, 'col', 'row'), may hold values from -0.3 to 1.3
- cofactor: float32 [4, 16, 256, 256], P(None, 'col', 'row'), may hold values from -0.3 to 1.3
- rates: float32 [4, 16, 256], P(None, 'col'), may hold values from 0.5 to 2
Outputs:
- updated_state: float32 [8192, 16, 1024], P('row', 'col')
Inputs may be any that keep to these rules, and one draw needn't show every extreme that they name: coupling and coupling_t hold the same matrix A; its blocks A(i, k) are zero unless k > i. coupling_t holds the transposed blocks of the A in coupling.
All inputs are finite; a program needn't handle non-finite values.
Results may differ from a plain program's by a relative error of at most 0.0003.
Values may be sent and summed in bfloat16 or wider, within the bound.
A program may use at most 64 MiB of HBM per device.

v0:
```python
import jax
import jax.numpy as jnp
from jax import lax
from jax.sharding import PartitionSpec as P

STEPS = 2


HIGHEST_PRECISION = lax.Precision.HIGHEST


def side_by_side(arrays, axis, dim, along):
    both = jnp.concatenate(arrays, axis=along)
    filled, at, finished = (lax.all_gather(both, axis, axis=dim, tiled=True), 0, [])
    for a in arrays:
        finished.append(lax.slice_in_dim(filled, at, at + a.shape[along], axis=along))
        at += a.shape[along]
    return tuple(finished)


def broadcast(value, axis, root):
    return lax.dynamic_index_in_dim(lax.all_gather(value, axis), root, 0, keepdims=False)


def from_behind(block, axis, distance):
    devices = range(lax.axis_size(axis))
    route = [((i - distance) % len(devices), i) for i in devices]
    return lax.ppermute(block, axis, route)


def solve_block(residual, left_p, left_q, left_e, right_p, right_q, right_e):
    middle = jnp.dot(
        left_q, residual, precision=HIGHEST_PRECISION, preferred_element_type=jnp.float32
    )
    middle = jnp.dot(
        middle, right_q.T, precision=HIGHEST_PRECISION, preferred_element_type=jnp.float32
    )
    middle = middle / (left_e[:, None] + right_e[None, :])
    product = jnp.dot(
        left_p, middle, precision=HIGHEST_PRECISION, preferred_element_type=jnp.float32
    )
    return -jnp.dot(
        product, right_p.T, precision=HIGHEST_PRECISION, preferred_element_type=jnp.float32
    )


def pick_slot(stacked, slot_index):
    return lax.dynamic_index_in_dim(stacked, slot_index, 0, keepdims=False)


def on_device(state, coupling, coupling_t, factor, cofactor, rates):
    row_count = lax.axis_size("row")
    col_count = lax.axis_size("col")
    half_rows = row_count // 2
    order_blocks = 2 * row_count
    col_slots = order_blocks // col_count
    block_size = state.shape[0]
    row_index = lax.axis_index("row")
    col_index = lax.axis_index("col")
    blocks = jnp.transpose(state.reshape(block_size, col_slots, block_size), (1, 0, 2))
    full_p, full_q = side_by_side((factor, cofactor), "row", 2, 0)
    right_ps = full_p.reshape(col_slots, block_size, block_size)
    right_qs = full_q.reshape(col_slots, block_size, block_size)
    right_es = rates.reshape(col_slots, block_size)
    own_slot = row_index // col_count
    picked = (
        pick_slot(right_ps, own_slot),
        pick_slot(right_qs, own_slot),
        pick_slot(right_es, own_slot),
    )
    left_p, left_q, left_e = (
        broadcast(picked[0], "col", row_index % col_count),
        broadcast(picked[1], "col", row_index % col_count),
        broadcast(picked[2], "col", row_index % col_count),
    )
    upper_row = coupling.reshape(block_size, col_slots * block_size)
    lower_pair = coupling_t.reshape(2, block_size, col_slots * block_size)
    my_columns = col_index + col_count * jnp.arange(col_slots, dtype=jnp.int32)
    upper_now = upper_row
    for wave_step in range(STEPS):
        antidiag = order_blocks - 1 - wave_step
        partner = antidiag - row_index
        owner_col = partner % col_count
        slot_here = partner // col_count
        usable = row_index <= partner
        residual = pick_slot(blocks, slot_here)
        solution = solve_block(
            residual,
            left_p,
            left_q,
            left_e,
            pick_slot(right_ps, slot_here),
            pick_slot(right_qs, slot_here),
            pick_slot(right_es, slot_here),
        )
        solution = jnp.where(usable, solution, 0.0)
        written = jnp.where(usable & (col_index == owner_col), solution, residual)
        blocks = lax.dynamic_update_index_in_dim(blocks, written, slot_here, 0)
        shared = broadcast(solution, "col", owner_col)
        mirror = antidiag - my_columns
        use_row = mirror <= my_columns
        sources = jnp.clip(jnp.where(use_row, mirror, my_columns), 0, row_count - 1)
        fetched = []
        for slot_index in range(col_slots):
            fetched.append(broadcast(shared, "row", sources[slot_index]))
        fetched = jnp.stack(fetched)
        partner_blocks = jnp.where(use_row[:, None, None], fetched, jnp.swapaxes(fetched, 1, 2))
        if wave_step > 0:
            upper_now = from_behind(upper_row, "col", (col_count - wave_step) % col_count)
        receiver = (row_index - wave_step - half_rows) % row_count
        send_slot = jnp.where(receiver + wave_step >= row_count, 1, 0)
        send_piece = pick_slot(lower_pair, send_slot)
        lower_now = from_behind(send_piece, "row", (half_rows - wave_step) % row_count)
        upper_view = upper_now.reshape(block_size, col_slots, block_size)
        rolled = jnp.where(
            (col_index + wave_step) // col_count == 1, jnp.roll(upper_view, -1, axis=1), upper_view
        )
        lower_view = lower_now.reshape(block_size, col_slots, block_size)
        left_terms = jnp.einsum(
            "aub,ubc->uac", rolled.astype(jnp.float32), partner_blocks, precision=HIGHEST_PRECISION
        )
        right_terms = jnp.einsum(
            "ab,buc->uac", shared, lower_view.astype(jnp.float32), precision=HIGHEST_PRECISION
        )
        targets = (row_index <= my_columns) & (row_index + my_columns < antidiag)
        blocks = blocks - jnp.where(targets[:, None, None], left_terms + right_terms, 0.0)
    return jnp.transpose(blocks, (1, 0, 2)).reshape(block_size, 1, col_slots * block_size)


def solution(mesh):
    return jax.shard_map(
        on_device,
        mesh=mesh,
        in_specs=(
            P("row", "col", None),
            P("row", "col", None),
            P(None, "row", "col", None),
            P(None, "col", "row", None),
            P(None, "col", "row", None),
            P(None, "col", None),
        ),
        out_specs=P("row", "col", None),
        check_vma=False,
    )
```

profile of v0, /device:TPU:1, one launch (start us, length us, event | category | flops | bytes accessed | tf_op | source)
XLA Modules:
  0.0 536.6 jit_solution(2571348042180677186)
XLA Ops:
  6.5 1.5 pad_maximum_fusion.2
  8.1 0.0 all-gather.21.cloned.1.call-start
  8.1 83.7 %all-gather.13.cloned.1.call-done = f32[8,1,256,256]{3,2,1,0:T(8,128)} async-done(((f32[8,1,8,256]{3,2,1,0:T(8,128)}), f32[8,1,256,256]{3,2,1,0:T(8,128)}) %all-gather.13.cloned.1.call-update) | async-done | bytes 2097168 | tf_op jit(solution)/shard_map/all_gather | solution.py:14
  91.9 1.7 fusion.55
  93.6 1.0 copy-done.6
  94.5 0.7 constant_dynamic-slice_fusion.15
  95.3 0.0 all-gather.19.cloned.1.call-start
  95.3 0.7 constant_dynamic-slice_fusion.16
  96.1 0.0 all-gather.23.cloned.1.call-start
  96.2 1.0 copy.33
  97.1 0.1 copy.65
  97.3 22.1 %all-gather.2 = f32[16,1,256]{2,1,0:T(1,128)S(1)} all-gather(f32[1,1,256]{2,1,0:T(1,128)S(1)} %get-tuple-element.18), channel_id=4, replica_groups=mesh['row'=32,'col'=16] {'col'}, dimensions={0}, use_global_device_ids=true | all-gather | bytes 17408 | tf_op jit(solution)/shard_map/all_gather | solution.py:22
  119.4 24.6 %all-gather.21.cloned.1.call-done = f32[16,1,256,256]{3,2,1,0:T(8,128)} async-done(((f32[1,1,256,256]{3,2,1,0:T(8,128)}), f32[16,1,256,256]{3,2,1,0:T(8,128)}) %all-gather.21.cloned.1.call-update) | async-done | bytes 4194320 | tf_op jit(solution)/shard_map/all_gather | solution.py:22
  144.0 1.4 fusion.24
  145.3 1.4 convolution_divide_fusion.1
  146.7 42.8 %all-gather.19.cloned.1.call-done = f32[16,1,256,256]{3,2,1,0:T(8,128)} async-done(((f32[1,1,256,256]{3,2,1,0:T(8,128)}), f32[16,1,256,256]{3,2,1,0:T(8,128)}) %all-gather.19.cloned.1.call-update) | async-done | bytes 4194320 | tf_op jit(solution)/shard_map/all_gather | solution.py:22
  189.5 1.3 fusion.30
  190.8 1.1 bitcast_dynamic-update-slice_fusion.1
  192.1 43.3 %all-gather.23.cloned.1.call-done = f32[4096,256]{0,1:T(8,128)} async-done(((f32[256,256]{0,1:T(8,128)}), f32[4096,256]{0,1:T(8,128)}) %all-gather.23.cloned.1.call-update) | async-done | bytes 4194320 | tf_op jit(solution)/shard_map/all_gather | solution.py:22
  235.4 5.7 %copy.51 = f32[4096,256]{1,0:T(8,128)} copy(f32[4096,256]{0,1:T(8,128)} %all-gather.23.cloned.1.call-done) | data formatting | bytes 8388608 | tf_op jit(solution)/shard_map/all_gather | solution.py:22
  241.1 1.7 constant_dynamic-slice_fusion.11
  242.9 1.1 dynamic-slice_bitcast_fusion
  243.9 7.1 %collective-permute-start = (bf16[256,1024]{1,0:T(8,128)(2,1)}, bf16[256,1024]{1,0:T(8,128)(2,1)}, u32[]{:S(2)}, u32[]{:S(2)}) collective-permute-start(bf16[256,1024]{1,0:T(8,128)(2,1)} %get-tuple-element.16), channel_id=1, source_target_pairs={{256,0},{272,16},{288,32},{304,48},{320,64},{336,80},{352,96},{368... | collective-permute-start | bytes 1572872 | tf_op jit(solution)/shard_map/ppermute | solution.py:28
  251.1 0.6 fusion.57
  256.6 0.4 reshape_reshape.3
  257.0 0.2 slice.61
  257.2 0.3 slice.60
  257.5 0.8 copy.63
  260.8 0.6 subtract_compare_fusion.1
  261.4 11.7 %collective-permute-done = bf16[256,1024]{1,0:T(8,128)(2,1)} collective-permute-done((bf16[256,1024]{1,0:T(8,128)(2,1)}, bf16[256,1024]{1,0:T(8,128)(2,1)}, u32[]{:S(2)}, u32[]{:S(2)}) %collective-permute-start) | collective-permute-done | bytes 524320 | tf_op jit(solution)/shard_map/ppermute | solution.py:28
  273.0 1.3 copy.40
  274.3 73.2 %all-gather.15.cloned.1.call-done = f32[32,256,256]{2,1,0:T(8,128)} async-done(((f32[1,256,256]{2,1,0:T(8,128)}), f32[32,256,256]{2,1,0:T(8,128)}) %all-gather.15.cloned.1.call-update) | async-done | bytes 8388624 | tf_op jit(solution)/shard_map/all_gather | solution.py:22
  347.5 1.3 constant_dynamic-slice_fusion.10
  348.8 0.7 copy-done.9
  349.4 0.1 copy-done.10
  349.6 0.1 copy-done.11
  349.6 0.1 copy-done.12
  349.7 0.1 pad_maximum_fusion
  349.8 1.3 copy.38
  351.1 2.8 fusion.7
  353.9 0.7 fusion.4
  354.7 1.4 fusion.19
  356.0 1.4 convolution_divide_fusion
  357.4 1.3 fusion.28
  358.7 2.1 bitcast_dynamic-update-slice_fusion
  360.9 43.9 %all-gather.25.cloned.1.call-done = f32[4096,256]{0,1:T(8,128)} async-done(((f32[256,256]{0,1:T(8,128)}), f32[4096,256]{0,1:T(8,128)}) %all-gather.25.cloned.1.call-update) | async-done | bytes 4194320 | tf_op jit(solution)/shard_map/all_gather | solution.py:22
  404.8 5.7 %copy.52 = f32[4096,256]{1,0:T(8,128)} copy(f32[4096,256]{0,1:T(8,128)} %all-gather.25.cloned.1.call-done) | data formatting | bytes 8388608 | tf_op jit(solution)/shard_map/all_gather | solution.py:22
  410.5 1.7 constant_dynamic-slice_fusion.4
  412.2 0.3 collective-permute-start.1
  412.5 7.1 %collective-permute-start.2 = (bf16[256,1024]{1,0:T(8,128)(2,1)S(1)}, bf16[256,1024]{1,0:T(8,128)(2,1)S(1)}, u32[]{:S(2)}, u32[]{:S(2)}) collective-permute-start(bf16[256,1024]{1,0:T(8,128)(2,1)S(1)} %copy-done.15), channel_id=1, source_target_pairs={{272,0},{288,16},{304,32},{320,48},{336,64},{352,80},{368,96},{384... | collective-permute-start | bytes 1572872 | tf_op jit(solution)/shard_map/ppermute | solution.py:28
  419.6 0.7 fusion.56
  427.9 0.9 slice.62
  428.7 22.2 %collective-permute-done.2 = bf16[256,1024]{1,0:T(8,128)(2,1)S(1)} collective-permute-done((bf16[256,1024]{1,0:T(8,128)(2,1)S(1)}, bf16[256,1024]{1,0:T(8,128)(2,1)S(1)}, u32[]{:S(2)}, u32[]{:S(2)}) %collective-permute-start.2) | collective-permute-done | bytes 524320 | tf_op jit(solution)/shard_map/ppermute | solution.py:28
  450.9 0.2 copy.47
  451.1 1.6 convolution_bitcast_fusion
  452.7 68.8 %all-gather.17.cloned.1.call-done = f32[32,256,256]{2,1,0:T(8,128)} async-done(((f32[1,256,256]{2,1,0:T(8,128)}), f32[32,256,256]{2,1,0:T(8,128)}) %all-gather.17.cloned.1.call-update) | async-done | bytes 8388624 | tf_op jit(solution)/shard_map/all_gather | solution.py:22
  521.4 1.3 constant_dynamic-slice_fusion.3
  522.7 0.7 copy-done.2
  523.4 0.1 copy-done.3
  523.5 0.1 copy-done.4
  523.6 0.1 pad_maximum_fusion.1
  523.7 1.3 copy.45
  525.0 2.9 fusion.1
  527.9 1.9 copy.48
  (47 shorter events, 0.4 us)
Async XLA Ops:
  6.5 89.6 %copy-start.7 = (f32[256,1,1024]{2,1,0:T(1,128)S(1)}, f32[256,1,1024]{2,1,0:T(1,128)}, u32[]{:S(2)}) copy-start(f32[256,1,1024]{2,1,0:T(1,128)} %param.6) | copy-start | bytes 3145732
  6.5 85.4 %all-gather.13.cloned.1.call-start = ((), (), s32[]{:S(2)}) async-start(), calls=%async_computation | async-start | bytes 2162688 | tf_op jit(solution)/shard_map/all_gather | solution.py:14
  8.1 135.9 %all-gather.21.cloned.1.call-start = ((), (), s32[]{:S(2)}) async-start(), calls=%async_computation.4 | async-start | bytes 4456448 | tf_op jit(solution)/shard_map/all_gather | solution.py:22
  8.1 89.1 %copy-start.16 = (f32[4,1,256]{2,1,0:T(1,128)S(1)}, f32[4,1,256]{2,1,0:T(1,128)}, u32[]{:S(2)}) copy-start(f32[4,1,256]{2,1,0:T(1,128)} %param.11) | copy-start | bytes 12292
  93.6 1.0 copy-start.6
  93.6 97.3 %copy-start = (f32[4,1,256,256]{3,2,1,0:T(8,128)}, f32[4,1,256,256]{3,2,1,0:T(8,128)S(1)}, u32[]{:S(2)}) copy-start(f32[4,1,256,256]{3,2,1,0:T(8,128)S(1)} %get-tuple-element.13) | copy-start | bytes 3145732
  95.3 94.2 %all-gather.19.cloned.1.call-start = ((), (), s32[]{:S(2)}) async-start(), calls=%async_computation.3 | async-start | bytes 4456448 | tf_op jit(solution)/shard_map/all_gather | solution.py:22
  96.1 139.3 %all-gather.23.cloned.1.call-start = ((), (), s32[]{:S(2)}) async-start(), calls=%async_computation.5 | async-start | bytes 4456448 | tf_op jit(solution)/shard_map/all_gather | solution.py:22
  192.0 155.5 %all-gather.15.cloned.1.call-start = ((), (), s32[]{:S(2)}) async-start(), calls=%async_computation.1 | async-start | bytes 8650752 | tf_op jit(solution)/shard_map/all_gather | solution.py:22
  192.1 50.8 %copy-start.8 = (bf16[2,256,1,1024]{3,1,2,0:T(8,128)(2,1)S(1)}, bf16[2,256,1,1024]{3,1,2,0:T(8,128)(2,1)}, u32[]{:S(2)}) copy-start(bf16[2,256,1,1024]{3,1,2,0:T(8,128)(2,1)} %param.8) | copy-start | bytes 3145732
  192.1 64.5 %copy-start.13 = (bf16[256,1,1024]{2,0,1:T(8,128)(2,1)S(1)}, bf16[256,1,1024]{2,0,1:T(8,128)(2,1)}, u32[]{:S(2)}) copy-start(bf16[256,1,1024]{2,0,1:T(8,128)(2,1)} %param.7) | copy-start | bytes 1572868
  242.8 162.1 %all-gather.25.cloned.1.call-start = ((), (), s32[]{:S(2)}) async-start(), calls=%async_computation.6 | async-start | bytes 4456448 | tf_op jit(solution)/shard_map/all_gather | solution.py:22
  243.9 29.1 %collective-permute-start = (bf16[256,1024]{1,0:T(8,128)(2,1)}, bf16[256,1024]{1,0:T(8,128)(2,1)}, u32[]{:S(2)}, u32[]{:S(2)}) collective-permute-start(bf16[256,1024]{1,0:T(8,128)(2,1)} %get-tuple-element.16), channel_id=1, source_target_pairs={{256,0},{272,16},{288,32},{304,48},{320,64},{336,80},{352,96},{368... | collective-permute-start | bytes 1572872 | tf_op jit(solution)/shard_map/ppermute | solution.py:28
  348.7 0.7 copy-start.9
  348.8 0.8 copy-start.10
  348.8 0.9 copy-start.11
  348.8 1.0 copy-start.12
  349.7 4.2 copy-start.1
  360.8 160.6 %all-gather.17.cloned.1.call-start = ((), (), s32[]{:S(2)}) async-start(), calls=%async_computation.2 | async-start | bytes 8650752 | tf_op jit(solution)/shard_map/all_gather | solution.py:22
  360.9 51.3 %copy-start.14 = (bf16[256,1,1024]{2,0,1:T(8,128)(2,1)S(1)}, bf16[256,1,1024]{2,0,1:T(8,128)(2,1)}, u32[]{:S(2)}) copy-start(bf16[256,1,1024]{2,0,1:T(8,128)(2,1)} %param.7) | copy-start | bytes 1572868
  360.9 51.6 %copy-start.15 = (bf16[256,1024]{1,0:T(8,128)(2,1)S(1)}, bf16[256,1024]{1,0:T(8,128)(2,1)}, u32[]{:S(2)}) copy-start(bf16[256,1024]{1,0:T(8,128)(2,1)} %get-tuple-element.15) | copy-start | bytes 1572868
  412.2 15.5 %collective-permute-start.1 = (bf16[256,1024]{1,0:T(8,128)(2,1)S(1)}, bf16[256,1024]{1,0:T(8,128)(2,1)S(1)}, u32[]{:S(2)}, u32[]{:S(2)}) collective-permute-start(bf16[256,1024]{1,0:T(8,128)(2,1)S(1)} %bitcast.121), channel_id=1, source_target_pairs={{1,0},{2,1},{3,2},{4,3},{5,4},{6,5},{7,6},{8,7},{9,8},{10,9},{11,1... | collective-permute-start | bytes 1572872 | tf_op jit(solution)/shard_map/ppermute | solution.py:28
  412.5 38.4 %collective-permute-start.2 = (bf16[256,1024]{1,0:T(8,128)(2,1)S(1)}, bf16[256,1024]{1,0:T(8,128)(2,1)S(1)}, u32[]{:S(2)}, u32[]{:S(2)}) collective-permute-start(bf16[256,1024]{1,0:T(8,128)(2,1)S(1)} %copy-done.15), channel_id=1, source_target_pairs={{272,0},{288,16},{304,32},{320,48},{336,64},{352,80},{368,96},{384... | collective-permute-start | bytes 1572872 | tf_op jit(solution)/shard_map/ppermute | solution.py:28
  427.8 0.9 copy-start.5
  522.7 0.7 copy-start.2
  522.7 0.8 copy-start.3
  522.7 0.9 copy-start.4
Sparse Core Ops, SparseCore 0:
  10.4 81.4 all-gather.12
  95.4 48.5 all-gather.20
  146.1 43.3 all-gather.18
  192.1 43.2 all-gather.22
  242.9 104.5 all-gather.14
  361.0 43.8 all-gather.24
  412.3 109.0 all-gather.16
where the time goes:
time: 538 us; the launch traced here: 537 us
  waiting for transfers between devices  414 us (77%)
  local copies, waits for them, and re-layouts  35.2 us (7%)
  between operations  28.9 us (5%)
  blocking collectives  22.1 us (4%)
  matrix products  19.2 us (4%)
  starting transfers between devices  14.7 us (3%)
    all_gather x6, waiting for transfers between devices, broadcast(): lax.all_gather(value, axis)  297 us
    all_gather x1, waiting for transfers between devices, side_by_side(): lax.all_gather(both, axis, axis=dim, tiled=True)  83.7 us
    ppermute x3, waiting for transfers between devices, from_behind(): return lax.ppermute(block, axis, route)  33.8 us
    all_gather x1, blocking collectives, broadcast(): lax.all_gather(value, axis)  22.1 us
    ppermute x3, starting transfers between devices, from_behind(): return lax.ppermute(block, axis, route)  14.5 us
    all_gather x2, local copies, waits for them, and re-layouts, broadcast(): lax.all_gather(value, axis)  11.4 us
  transfers between devices with their start and end apart: 10, of which 9 were waited for; matrix products, arithmetic and copies ran while one was open for 2% of the time, Pallas kernels for 0%

commit v1 on v0

v1 whole, which is shorter than its diff:
```python
import functools

import jax
import jax.numpy as jnp
from jax import lax
from jax.experimental import pallas as pl
from jax.experimental.pallas import tpu as pltpu
from jax.sharding import PartitionSpec as P

MESH = pl.DeviceIdType.MESH
STEPS = 2
XS = 4
BS = 256


def split2(a):
    hi = a.astype(jnp.bfloat16)
    return hi, (a - hi.astype(jnp.float32)).astype(jnp.bfloat16)


def nn(a, b):
    return lax.dot_general(a, b, (((1,), (0,)), ((), ())), preferred_element_type=jnp.float32)


def nt(a, b):
    return lax.dot_general(a, b, (((1,), (1,)), ((), ())), preferred_element_type=jnp.float32)


def dot3(dot, a, b):
    ah, al = split2(a)
    bh, bl = split2(b)
    return dot(ah, bh) + dot(ah, bl) + dot(al, bh)


def kernel(
    rows, cols, slots,
    st_in, cp_in, ct_in, p_in, q_in, e_in, out,
    st, w, a0, a1, at0, at1, pq, es, el, xr, zs,
    loc_sem, pq_ssem, pq_rsem, e_ssem, e_rsem,
    at_ssem, at0_rsem, atf_ssem, at1_rsem, a1_ssem, a1_rsem,
    xr_ssem, xr_rsem, z_ssem, z_rsem, root_ssem,
):
    r, c = lax.axis_index("row"), lax.axis_index("col")
    y, x = r // XS, lax.rem(r, XS)
    nb = 2 * rows
    pending = []

    def send(pred, src, dst, ssem, rsem, dev):
        cp = pltpu.make_async_remote_copy(
            src_ref=src, dst_ref=dst, send_sem=ssem, recv_sem=rsem,
            device_id=dev, device_id_type=MESH,
        )
        pl.when(pred)(cp.start)
        pending.append((pred, cp))

    def arrived(pred, dst, rsem):
        cp = pltpu.make_async_copy(dst, dst, rsem)
        pl.when(pred)(cp.wait)

    true = r >= 0
    sc = [lax.rem(nb - 1 - s - r, cols) for s in range(STEPS)]
    us = [(nb - 1 - s - r) // cols for s in range(STEPS)]
    is_s = [c == sc[s] for s in range(STEPS)]
    tcol, tslot = lax.rem(r, cols), r // cols

    ld_st = pltpu.make_async_copy(st_in, st, loc_sem.at[0])
    ld_st.start()
    ld_a0 = [
        pltpu.make_async_copy(cp_in.at[:, pl.ds(u * BS, BS)], a0.at[u], loc_sem.at[1 + u])
        for u in range(slots)
    ]
    for cp in ld_a0:
        cp.start()

    es[...] = jnp.broadcast_to(e_in[...], es.shape)

    def to_solver(s, side, q):
        if side == 0:
            m = c + cols * q
            slot = q
            dr, dc = m, lax.rem(nb - 1 - s - m, cols)
        else:
            m = c + cols * (2 + q)
            if s == 1:
                m = m - jnp.where(c == cols - 1, cols, 0)
            slot = m // cols
            dr, dc = nb - 1 - s - m, c
        mine = (dr == r) & (dc == c)
        for t, ref in enumerate((p_in, q_in)):
            src = ref.at[slot]
            dst = pq.at[s, side, t, pl.ds(pl.multiple_of(r * 8, 8), 8), :]
            send(~mine, src, dst, pq_ssem.at[s, side, q, t], pq_rsem.at[s, side], (dr, dc))
            pl.when(mine)(pltpu.make_async_copy(src, dst, pq_rsem.at[s, side]).start)

    def rate_to_solver(s):
        have = c == tcol
        mine = c == sc[s]
        send(have & ~mine, es.at[tslot], el.at[s], e_ssem.at[s], e_rsem.at[s], (r, sc[s]))
        pl.when(have & mine)(pltpu.make_async_copy(es.at[tslot], el.at[s], e_rsem.at[s]).start)

    for s in range(STEPS):
        for side in range(2):
            for q in range(2):
                to_solver(s, side, q)
        rate_to_solver(s)

    def at_needed(g, u):
        m = c + cols * u
        return (m >= g - 1) & (m <= nb - 2 - g)

    g = lax.rem(r + rows // 2, rows)
    for u in reversed(range(slots)):
        send(at_needed(g, u), ct_in.at[0, :, pl.ds(u * BS, BS)], at0.at[u],
             at_ssem.at[u], at0_rsem.at[u], (g, c))

    c_dn = lax.rem(c + cols - 1, cols)

    def step1_target(row, m):
        return (row <= m) & (row + m < nb - 2)

    for u in range(slots):
        wrap = jnp.where(c == 0, 1, 0)
        du = u - wrap
        send((du >= 0) & step1_target(r, c_dn + cols * du), cp_in.at[:, pl.ds(u * BS, BS)],
             a1.at[jnp.maximum(du, 0)], a1_ssem.at[u], a1_rsem.at[jnp.maximum(du, 0)], (r, c_dn))

    ld_st.wait()
    for u in range(slots):
        w[u] = st[:, 0, u * BS:(u + 1) * BS]
    for cp in ld_a0:
        cp.wait()

    def col_of(s, u):
        d = nb - 1 - s
        m = c + cols * u
        j = jnp.minimum(m, d - m)
        return d, m, j, m <= d

    def solver_sends(s):
        on = is_s[s]
        for h in range(2):
            if s == 0:
                send(on, xr.at[s, h], xr.at[s, h], xr_ssem.at[s, h, 3], xr_rsem.at[s, h], (r, sc[1]))
        for h in range(2):
            send(on & (c != tcol), xr.at[s, h], zs.at[s, tslot, h], root_ssem.at[s, h],
                 z_rsem.at[s, tslot, h], (r, tcol))

    def col_forward(s, u, on, wait=True):
        d, m, j, valid = col_of(s, u)
        yj, xj = j // XS, lax.rem(j, XS)
        root = valid & (r == j) & on
        own = is_s[s] & (u == us[s])
        if s == 1:
            own = own | (is_s[s] & (r == c + cols * u) & (c == tcol))
        holds = valid & (y <= yj) & on
        for h in range(2):
            buf, rs = zs.at[s, u, h], z_rsem.at[s, u, h]
            if wait:
                arrived(holds & ~own, buf, rs)

            def go(kind, pred, dev):
                send(pred, buf, buf, z_ssem.at[s, u, h, kind], rs, dev)

            direct = (u >= 2) if s == 0 else jnp.bool_(False)
            go(5, root & direct & (xj == 0) & (j >= 1), (jnp.maximum(j - 1, 0), c))
            for kind, dx in ((2, 3), (0, 1), (1, 2)):
                go(kind, root, (yj * XS + lax.rem(xj + dx, XS), c))
            dist = yj - y
            down = (dist >= 0) & (y >= 1) & (dist + 1 <= 4)
            skip = (dist == 0) & direct & (xj == 0) & (x == XS - 1)
            go(3, holds & down & ~skip, (jnp.maximum(r - XS, 0), c))
            first_up = (dist == 0) & (yj >= 5)
            next_up = (dist > 4) & (dist - 1 > 4)
            go(4, holds & (first_up | next_up), (jnp.where(first_up, x, lax.rem(r + XS, rows)), c))

    def row_forward(s):
        cs = sc[s]
        hz = lax.rem(c // 2 - cs // 2 + cols // 2, cols // 2)
        member = lax.rem(c, 2) == lax.rem(cs, 2)
        solver = is_s[s]
        mate = c + 1 - 2 * lax.rem(c, 2)
        early = is_s[1] if s == 0 else jnp.bool_(False)
        to_early = (mate == sc[1]) if s == 0 else jnp.bool_(False)
        half = cols // 4
        for h in range(2):
            arrived(~solver & ~early, xr.at[s, h], xr_rsem.at[s, h])

            def go(kind, pred, dc):
                send(pred, xr.at[s, h], xr.at[s, h], xr_ssem.at[s, h, kind], xr_rsem.at[s, h], (r, dc))

            go(0, member & (hz < half), lax.rem(c + 2, cols))
            go(1, member & ((hz == 0) | (hz > half + 1)), lax.rem(c + cols - 2, cols))
            go(2, member & ~to_early, mate)

    def solve(s):
        for side in range(2):
            pltpu.make_async_copy(pq.at[s, side], pq.at[s, side], pq_rsem.at[s, side]).wait()
        pltpu.make_async_copy(el.at[s], el.at[s], e_rsem.at[s]).wait()
        left_e = jnp.transpose(el[s])[:, :1]
        right_e = e_in[us[s]]
        mid = dot3(nn, pq[s, 0, 1], w[us[s]])
        mid = dot3(nt, mid, pq[s, 1, 1])
        mid = mid / (left_e + right_e)
        mid = dot3(nn, pq[s, 0, 0], mid)
        sol = -dot3(nt, mid, pq[s, 1, 0])
        hi, lo = split2(sol)
        xr[s, 0] = hi
        xr[s, 1] = lo
        if s == 0:
            zs[s, us[s], 0] = hi
            zs[s, us[s], 1] = lo
        else:
            last = r == rows - 1

            @pl.when(last)
            def _():
                th, tl = split2(jnp.transpose(sol))
                zs[s, us[s], 0] = th
                zs[s, us[s], 1] = tl

            @pl.when(~last)
            def _():
                zs[s, us[s], 0] = hi
                zs[s, us[s], 1] = lo

            @pl.when(~last & (c == tcol))
            def _():
                zs[s, tslot, 0] = hi
                zs[s, tslot, 1] = lo
        w[us[s]] = sol

    def terms(s, a, u, at, dot):
        z = zs.at[s, u]
        return dot(a, z[0]) + dot(a, z[1]) + nn(xr[s, 0], at) + nn(xr[s, 1], at)

    pl.when(is_s[0])(functools.partial(solve, 0))
    solver_sends(0)
    col_forward(0, us[0], is_s[0], wait=False)

    u1 = us[1]
    for h in range(2):
        arrived(is_s[1], xr.at[0, h], xr_rsem.at[0, h])
    col_forward(0, u1, is_s[1])
    arrived(is_s[1], at0.at[u1], at0_rsem.at[u1])

    @pl.when(is_s[1] & (r == rows - 1))
    def _():
        w[u1] = w[u1] - terms(0, a0[u1], u1, at0[u1], nt)

    @pl.when(is_s[1] & (r < rows - 1))
    def _():
        w[u1] = w[u1] - terms(0, a0[u1], u1, at0[u1], nn)

    pl.when(is_s[1])(functools.partial(solve, 1))
    solver_sends(1)
    col_forward(1, u1, is_s[1], wait=False)

    for u in reversed(range(slots)):
        arrived(at_needed(r, u) & ~(is_s[1] & (u == u1)), at0.at[u], at0_rsem.at[u])
        send(at_needed(r, u) & (r >= 1), at0.at[u], at1.at[u], atf_ssem.at[u], at1_rsem.at[u],
             (jnp.maximum(r - 1, 0), c))

    def update(s, a_ref, at_ref):
        for u in range(slots):
            m = c + cols * u
            target = (r <= m) & (r + m < nb - 1 - s)
            if s == 0:
                target = target & ~(is_s[1] & (u == u1))

            @pl.when(target)
            def _(u=u):
                w[u] = w[u] - terms(s, a_ref[u], u, at_ref[u], nt if u < 2 else nn)

    row_forward(0)
    for u in (2, 3, 1, 0):
        handled = (is_s[0] & (u == us[0])) | (is_s[1] & (u == u1))
        col_forward(0, u, ~handled)
    update(0, a0, at0)

    for u in (2, 3):
        col_forward(1, u, ~(is_s[1] & (u == u1)))
    row_forward(1)
    for u in (1, 0):
        col_forward(1, u, ~(is_s[1] & (u == u1)))
    for u in range(slots):
        need = step1_target(r, c + cols * u)
        arrived(need, a1.at[u], a1_rsem.at[u])
        arrived(at_needed(r + 1, u) & (r < rows - 1), at1.at[u], at1_rsem.at[u])
    update(1, a1, at1)
    for u in range(slots):
        out[:, 0, u * BS:(u + 1) * BS] = w[u]

    for pred, cp in pending:
        pl.when(pred)(cp.wait_send)


def solution(mesh):
    rows, cols = mesh.shape["row"], mesh.shape["col"]

    def on_device(state, coupling, coupling_t, factor, cofactor, rates):
        slots = 2 * rows // cols
        width = slots * BS
        any_space = pl.BlockSpec(memory_space=pl.ANY)
        vmem = pl.BlockSpec(memory_space=pltpu.VMEM)
        f32, bf16 = jnp.float32, jnp.bfloat16
        dma = pltpu.SemaphoreType.DMA
        return pl.pallas_call(
            functools.partial(kernel, rows, cols, slots),
            out_shape=jax.ShapeDtypeStruct((BS, 1, width), f32),
            in_specs=[any_space] * 5 + [vmem],
            out_specs=vmem,
            scratch_shapes=[
                pltpu.VMEM((BS, 1, width), f32),
                pltpu.VMEM((slots, BS, BS), f32),
                pltpu.VMEM((slots, BS, BS), bf16),
                pltpu.VMEM((slots, BS, BS), bf16),
                pltpu.VMEM((slots, BS, BS), bf16),
                pltpu.VMEM((slots, BS, BS), bf16),
                pltpu.VMEM((STEPS, 2, 2, BS, BS), f32),
                pltpu.VMEM((slots, 8, BS), f32),
                pltpu.VMEM((STEPS, 8, BS), f32),
                pltpu.VMEM((STEPS, 2, BS, BS), bf16),
                pltpu.VMEM((STEPS, slots, 2, BS, BS), bf16),
                dma((1 + slots,)),
                dma((STEPS, 2, 2, 2)),
                dma((STEPS, 2)),
                dma((STEPS,)),
                dma((STEPS,)),
                dma((slots,)),
                dma((slots,)),
                dma((slots,)),
                dma((slots,)),
                dma((slots,)),
                dma((slots,)),
                dma((STEPS, 2, 4)),
                dma((STEPS, 2)),
                dma((STEPS, slots, 2, 6)),
                dma((STEPS, slots, 2)),
                dma((STEPS, 2)),
            ],
            compiler_params=pltpu.CompilerParams(
                has_side_effects=True, vmem_limit_bytes=40 * 1024 * 1024
            ),
        )(
            state,
            coupling.reshape(BS, width),
            coupling_t.reshape(2, BS, width),
            factor.reshape(slots, 8, BS),
            cofactor.reshape(slots, 8, BS),
            rates,
        )

    return jax.shard_map(
        on_device,
        mesh=mesh,
        in_specs=(
            P("row", "col", None),
            P("row", "col", None),
            P(None, "row", "col", None),
            P(None, "col", "row", None),
            P(None, "col", "row", None),
            P(None, "col", None),
        ),
        out_specs=P("row", "col", None),
        check_vma=False,
    )
```

time: 538 us -> 162 us (0.30)
  the two profiles are of different devices: /device:TPU:1 before, /device:TPU:67 now
where the time goes in v1:
time: 162 us
  Pallas kernels  155 us (96%)
  local copies, waits for them, and re-layouts  6.66 us (4%)
    pallas_call x1, Pallas kernels, on_device(): pl.pallas_call(functools.partial(kernel, rows, cols, slots), out_shape=ja...  155 us
    unnamed x13, local copies, waits for them, and re-layouts  6.66 us

profile of v1, /device:TPU:67, one launch (start us, length us, event | category | flops | bytes accessed | tf_op | source)
XLA Modules:
  0.0 162.0 jit_solution(11504595552988819012)
XLA Ops:
  0.0 0.0 copy-start.5
  0.0 0.7 copy-done.5
  0.7 0.0 copy-start
  0.7 1.2 copy-done
  1.9 0.0 copy-start.1
  1.9 1.2 copy-done.1
  3.1 0.0 copy-start.2
  3.1 1.0 copy-done.2
  4.2 0.0 copy-start.3
  4.2 0.8 copy-done.3
  4.9 0.0 copy-start.4
  4.9 0.8 copy-done.4
  5.7 155.4 %shard_map.64 = f32[256,1,1024]{2,1,0:T(1,128)S(1)} custom-call(f32[256,1,1024]{2,1,0:T(1,128)S(1)} %copy-done, bf16[256,1024]{1,0:T(8,128)(2,1)S(1)} %bitcast.5, bf16[2,256,1024]{2,1,0:T(8,128)(2,1)S(1)} %bitcast.4, f32[4,8,256]{2,1,0:T(8,128)S(1)} %bitcast.6, f32[4,8,256]{2,1,0:T(8,128)S(1)} %bitcast.7, f32[4,1,256]{2,1,0:T(1,128)S(1)} %copy-done.5), custom_call_target="tpu_custom_call" | custom-call | tf_op jit(solution)/shard_map/pallas_call | solution.py:307
  161.1 1.0 copy.8
Async XLA Ops:
  0.0 0.7 copy-start.5
  0.7 1.2 copy-start
  1.9 1.2 copy-start.1
  3.1 1.0 copy-start.2
  4.2 0.8 copy-start.3
  4.9 0.8 copy-start.4

commit v2 on v1

v2 whole, which is shorter than its diff:
```python
import functools

import jax
import jax.numpy as jnp
from jax import lax
from jax.experimental import pallas as pl
from jax.experimental.pallas import tpu as pltpu
from jax.sharding import PartitionSpec as P

MESH = pl.DeviceIdType.MESH
STEPS = 2
XS = 4
BS = 256


def split2(a):
    hi = a.astype(jnp.bfloat16)
    return hi, (a - hi.astype(jnp.float32)).astype(jnp.bfloat16)


def nn(a, b):
    return lax.dot_general(a, b, (((1,), (0,)), ((), ())), preferred_element_type=jnp.float32)


def nt(a, b):
    return lax.dot_general(a, b, (((1,), (1,)), ((), ())), preferred_element_type=jnp.float32)


def dot3(dot, a, b):
    ah, al = split2(a)
    bh, bl = split2(b)
    return dot(ah, bh) + dot(ah, bl) + dot(al, bh)


def kernel(
    rows, cols, slots,
    st_in, cp_in, ct_in, p_in, q_in, e_in, out,
    st, w, a0, a1, at0, at1, pq, ev, es, el, xr, zs,
    loc_sem, pq_ssem, pq_rsem, e_ssem, e_rsem,
    at_ssem, at0_rsem, atf_ssem, at1_rsem, a1_ssem, a1_rsem,
    xr_ssem, xr_rsem, z_ssem, z_rsem, sv_ssem, er_ssem,
):
    r, c = lax.axis_index("row"), lax.axis_index("col")
    y, x = r // XS, lax.rem(r, XS)
    nb = 2 * rows
    pending = []

    def send(pred, src, dst, ssem, rsem, dev):
        cp = pltpu.make_async_remote_copy(
            src_ref=src, dst_ref=dst, send_sem=ssem, recv_sem=rsem,
            device_id=dev, device_id_type=MESH,
        )
        pl.when(pred)(cp.start)
        pending.append((pred, cp))

    def arrived(pred, dst, rsem):
        cp = pltpu.make_async_copy(dst, dst, rsem)
        pl.when(pred)(cp.wait)

    sc = [lax.rem(nb - 1 - s - r, cols) for s in range(STEPS)]
    us = [(nb - 1 - s - r) // cols for s in range(STEPS)]
    is_s = [c == sc[s] for s in range(STEPS)]
    tcol, tslot = lax.rem(r, cols), r // cols

    barrier = pltpu.get_barrier_semaphore()

    def greet(dr, dc):
        pl.semaphore_signal(barrier, inc=1, device_id=(dr, dc), device_id_type=MESH)

    ys = rows // XS
    for dx in range(1, XS):
        greet(y * XS + lax.rem(x + dx, XS), c)
    for dy in range(1, ys):
        greet(lax.rem(r + dy * XS, rows), c)
    greet(lax.rem(r + 1, rows), c)
    for dz in range(1, cols // 2):
        greet(r, lax.rem(c + 2 * dz, cols))
    greet(r, lax.rem(c + 1, cols))
    greet(r, c + 1 - 2 * lax.rem(c, 2))
    expected = XS - 1 + ys - 1 + 1 + cols // 2 - 1 + 2
    tj = y * XS + lax.rem(c, XS)
    near = lax.rem(y, cols // XS) == c // XS
    for s in range(STEPS):
        tj_col = lax.rem(nb - 1 - s - tj, cols)
        alone = (tj == r) & (tj_col == c)

        @pl.when(near & ~alone)
        def _(tj_col=tj_col):
            greet(tj, tj_col)

        expected = expected + jnp.where(is_s[s], XS, 0) - jnp.where(is_s[s] & (c == tcol), 1, 0)

        @pl.when(is_s[s])
        def _():
            for k in range(1, rows):
                greet(lax.rem(r + k, rows), c)

            for k in range(1, rows):
                greet(lax.rem(r + k, rows), tcol)

            @pl.when(c != tcol)
            def _():
                greet(r, tcol)

        expected = expected + 4 - jnp.where(is_s[s], 1, 0) - jnp.where(is_s[s] & (c == tcol), 1, 0)

    ld_st = pltpu.make_async_copy(st_in, st, loc_sem.at[0])
    ld_st.start()
    ld_a0 = [
        pltpu.make_async_copy(cp_in.at[:, pl.ds(u * BS, BS)], a0.at[u], loc_sem.at[1 + u])
        for u in range(slots)
    ]
    for cp in ld_a0:
        cp.start()
    ld_e = pltpu.make_async_copy(e_in, ev, loc_sem.at[1 + slots])
    ld_e.start()
    ld_e.wait()
    es[...] = jnp.broadcast_to(ev[...], es.shape)
    with jax.named_scope("barrier"):
        pl.semaphore_wait(barrier, expected)

    def to_solver(s, side, q):
        if side == 0:
            m = c + cols * q
            slot = q
            dr, dc = m, lax.rem(nb - 1 - s - m, cols)
        else:
            m = c + cols * (2 + q)
            if s == 1:
                m = m - jnp.where(c == cols - 1, cols, 0)
            slot = m // cols
            dr, dc = nb - 1 - s - m, c
        mine = (dr == r) & (dc == c)
        for t, ref in enumerate((p_in, q_in)):
            src = ref.at[slot]
            dst = pq.at[s, side, t, pl.ds(pl.multiple_of(r * 8, 8), 8), :]
            send(~mine, src, dst, pq_ssem.at[s, side, q, t], pq_rsem.at[s, side], (dr, dc))
            pl.when(mine)(pltpu.make_async_copy(src, dst, pq_rsem.at[s, side]).start)

    def rate_to_solver(s):
        have = c == tcol
        mine = c == sc[s]
        send(have & ~mine, es.at[tslot], el.at[s], e_ssem.at[s], e_rsem.at[s], (r, sc[s]))
        pl.when(have & mine)(pltpu.make_async_copy(es.at[tslot], el.at[s], e_rsem.at[s]).start)

    for s in range(STEPS):
        for side in range(2):
            for q in range(2):
                to_solver(s, side, q)
        rate_to_solver(s)

    for pred, cp in pending:
        pl.when(pred)(cp.wait_send)
    pending.clear()

    def at_needed(g, u):
        m = c + cols * u
        return (m >= g - 1) & (m <= nb - 2 - g)

    g = lax.rem(r + rows // 2, rows)
    for u in reversed(range(slots)):
        send(at_needed(g, u), ct_in.at[0, :, pl.ds(u * BS, BS)], at0.at[u],
             at_ssem.at[u], at0_rsem.at[u], (g, c))

    c_dn = lax.rem(c + cols - 1, cols)

    def step1_target(row, m):
        return (row <= m) & (row + m < nb - 2)

    for u in range(slots):
        wrap = jnp.where(c == 0, 1, 0)
        du = u - wrap
        send((du >= 0) & step1_target(r, c_dn + cols * du), cp_in.at[:, pl.ds(u * BS, BS)],
             a1.at[jnp.maximum(du, 0)], a1_ssem.at[u], a1_rsem.at[jnp.maximum(du, 0)], (r, c_dn))

    with jax.named_scope("local_in"):
        ld_st.wait()
        for u in range(slots):
            w[u] = st[:, 0, u * BS:(u + 1) * BS]
        for cp in ld_a0:
            cp.wait()

    def col_of(s, u):
        d = nb - 1 - s
        m = c + cols * u
        j = jnp.minimum(m, d - m)
        return d, m, j, m <= d

    def quarter(ref, q):
        return ref.at[:, pl.ds(pl.multiple_of(q * (BS // XS), BS // XS), BS // XS), :]

    def place(s, u):
        d = nb - 1 - s
        m = c + cols * u
        j = jnp.minimum(m, d - m)
        yj, xj = j // XS, lax.rem(j, XS)
        own_root = jnp.bool_(u >= 2) if isinstance(u, int) else u >= 2
        if s == 1:
            own_root = own_root | (lax.rem(j, cols // 2) == cols // 2 - 1)
        early = (j - 1) if s == 0 else j - 2 * rows
        early = jnp.where(u >= 2, early, -2 * rows)
        return j, yj, xj, m <= d, own_root, early

    def needed(s, u, row):
        j, yj, xj, valid, own_root, _ = place(s, u)
        return valid & ((row < j) | ((row == j) & ~own_root))

    def solver_sends(s):
        on = is_s[s]
        own = zs.at[s, us[s]]
        early = r - 1 if s == 0 else r - 2 * rows
        for k, dx in enumerate((3, 1, 2)):
            q = lax.rem(x + dx, XS)
            row = y * XS + q
            send(on & (row != early), quarter(own, q), quarter(own, q), sv_ssem.at[s, k],
                 z_rsem.at[s, us[s], q], (row, c))
        for q in range(XS):
            row = y * XS + q
            mine = (c == tcol) & (x == q)
            if s == 1:
                mine = mine | (r == rows - 1)
            send(on & ~mine, quarter(xr.at[s], q), quarter(zs.at[s, tslot], q), sv_ssem.at[s, 3 + q],
                 z_rsem.at[s, tslot, q], (row, tcol))

    def early_sends():
        on = is_s[0]
        send(on, xr.at[0], xr.at[0], er_ssem.at[XS], xr_rsem.at[0], (r, sc[1]))
        own = zs.at[0, us[0]]
        for q in range(XS):
            send(on & (r >= 1), quarter(own, q), quarter(own, q), er_ssem.at[q],
                 z_rsem.at[0, us[0], q], (jnp.maximum(r - 1, 0), c))

    def relay(s, u, on):
        j, yj, xj, valid, own_root, early = place(s, u)
        part = quarter(zs.at[s, u], x)
        first = on & valid & (y == yj)
        for y2 in range(ys - 1):
            row = y2 * XS + x
            send(first & (y2 < yj) & (row != early), part, part, z_ssem.at[s, u, y2],
                 z_rsem.at[s, u, x], (row, c))
        for k, dx in enumerate((1, 3, 2)):
            row = y * XS + lax.rem(x + dx, XS)
            send(on & needed(s, u, row) & (row != early), part, part, z_ssem.at[s, u, ys - 1 + k],
                 z_rsem.at[s, u, x], (row, c))

    def own_part(s, u):
        own = is_s[s] & (u == us[s])
        if s == 1:
            own = own | (is_s[s] & (c == tcol) & (u == tslot))
        return own

    def done_early(s, u):
        done = own_part(s, u)
        if s == 0:
            done = done | (is_s[1] & (u == u1) & (r < rows - 1))
        return done

    def relays(s, first):
        for u in (3, 0, 2, 1):
            j, yj, xj, valid, own_root, early = place(s, u)
            on = valid & ((y == yj) if first else (y < yj)) & ~done_early(s, u)
            arrived(on, quarter(zs.at[s, u], x), z_rsem.at[s, u, x])
            relay(s, u, on)

    def rest(s, u):
        on = needed(s, u, r) & ~done_early(s, u)
        for k in range(1, XS):
            q = lax.rem(x + k, XS)
            arrived(on, quarter(zs.at[s, u], q), z_rsem.at[s, u, q])

    def row_sends(s):
        for dz in (4, 3, 5, 2, 6, 1, 7):
            send(is_s[s], xr.at[s], xr.at[s], xr_ssem.at[s, dz - 1], xr_rsem.at[s],
                 (r, lax.rem(c + 2 * dz, cols)))

    def row_relay(s):
        solver = is_s[s]
        early = is_s[1] if s == 0 else jnp.bool_(False)
        mate = c + 1 - 2 * lax.rem(c, 2)
        to_early = (mate == sc[1]) if s == 0 else jnp.bool_(False)
        member = lax.rem(c, 2) == lax.rem(sc[s], 2)
        arrived(~solver & ~early, xr.at[s], xr_rsem.at[s])
        send(member & ~to_early, xr.at[s], xr.at[s], xr_ssem.at[s, 7], xr_rsem.at[s], (r, mate))

    def solve(s):
        for side in range(2):
            with jax.named_scope(f"wait_pq{s}{side}"):
                pltpu.make_async_copy(pq.at[s, side], pq.at[s, side], pq_rsem.at[s, side]).wait()
        pltpu.make_async_copy(el.at[s], el.at[s], e_rsem.at[s]).wait()
        left_e = jnp.transpose(el[s])[:, :1]
        right_e = ev[us[s]]
        mid = dot3(nn, pq[s, 0, 1], w[us[s]])
        mid = dot3(nt, mid, pq[s, 1, 1])
        mid = mid / (left_e + right_e)
        mid = dot3(nn, pq[s, 0, 0], mid)
        sol = -dot3(nt, mid, pq[s, 1, 0])
        hi, lo = split2(sol)
        xr[s, 0] = hi
        xr[s, 1] = lo
        if s == 0:
            zs[s, us[s], 0] = hi
            zs[s, us[s], 1] = lo
        else:
            last = r == rows - 1

            @pl.when(last)
            def _():
                th, tl = split2(jnp.transpose(sol))
                zs[s, us[s], 0] = th
                zs[s, us[s], 1] = tl

            @pl.when(~last)
            def _():
                zs[s, us[s], 0] = hi
                zs[s, us[s], 1] = lo

            @pl.when(~last & (c == tcol))
            def _():
                zs[s, tslot, 0] = hi
                zs[s, tslot, 1] = lo
        w[us[s]] = sol

    def terms(z, s, a, at, dot):
        return dot(a, z[0]) + dot(a, z[1]) + nn(xr[s, 0], at) + nn(xr[s, 1], at)

    u1 = us[1]
    with jax.named_scope("solve0"):
        pl.when(is_s[0])(functools.partial(solve, 0))
    early_sends()
    solver_sends(0)
    relay(0, us[0], is_s[0])
    row_sends(0)

    with jax.named_scope("early_wait_xr"):
        arrived(is_s[1], xr.at[0], xr_rsem.at[0])
    with jax.named_scope("early_wait_z"):
        early_on = is_s[1] & (r < rows - 1)
        for q in range(XS):
            arrived(early_on, quarter(zs.at[0, u1], q), z_rsem.at[0, u1, q])
        relay(0, u1, early_on)
    with jax.named_scope("early_wait_at"):
        arrived(is_s[1], at0.at[u1], at0_rsem.at[u1])

    @pl.when(is_s[1] & (r == rows - 1))
    def _():
        w[u1] = w[u1] - terms(xr.at[0], 0, a0[u1], at0[u1], nt)

    @pl.when(early_on)
    def _():
        w[u1] = w[u1] - terms(zs.at[0, u1], 0, a0[u1], at0[u1], nn)

    with jax.named_scope("solve1"):
        pl.when(is_s[1])(functools.partial(solve, 1))
    solver_sends(1)
    relay(1, u1, is_s[1])
    relay(1, tslot, is_s[1] & (c == tcol) & (r < rows - 1))
    row_sends(1)

    with jax.named_scope("at_forward"):
        for u in reversed(range(slots)):
            arrived(at_needed(r, u) & ~(is_s[1] & (u == u1)), at0.at[u], at0_rsem.at[u])
            send(at_needed(r, u) & (r >= 1), at0.at[u], at1.at[u], atf_ssem.at[u], at1_rsem.at[u],
                 (jnp.maximum(r - 1, 0), c))

    def update(s, a_ref, at_ref):
        for u in range(slots):
            m = c + cols * u
            target = (r <= m) & (r + m < nb - 1 - s)
            if s == 0:
                target = target & ~(is_s[1] & (u == u1))

            @pl.when(target)
            def _(u=u):
                w[u] = w[u] - terms(zs.at[s, u], s, a_ref[u], at_ref[u], nt if u < 2 else nn)

    with jax.named_scope("relay0a"):
        relays(0, True)
    with jax.named_scope("relay0b"):
        relays(0, False)
    with jax.named_scope("row0"):
        row_relay(0)
    with jax.named_scope("relay1a"):
        relays(1, True)
    with jax.named_scope("rest0"):
        for u in range(slots):
            rest(0, u)
    with jax.named_scope("update0"):
        update(0, a0, at0)
    with jax.named_scope("relay1b"):
        relays(1, False)
    with jax.named_scope("row1"):
        row_relay(1)
    with jax.named_scope("rest1"):
        for u in range(slots):
            rest(1, u)
    with jax.named_scope("wait_a1_at1"):
        for u in range(slots):
            need = step1_target(r, c + cols * u)
            arrived(need, a1.at[u], a1_rsem.at[u])
            arrived(at_needed(r + 1, u) & (r < rows - 1), at1.at[u], at1_rsem.at[u])
    with jax.named_scope("update1"):
        update(1, a1, at1)
    with jax.named_scope("write_out"):
        for u in range(slots):
            out[:, 0, u * BS:(u + 1) * BS] = w[u]
    with jax.named_scope("drain"):
        for pred, cp in pending:
            pl.when(pred)(cp.wait_send)


def solution(mesh):
    rows, cols = mesh.shape["row"], mesh.shape["col"]

    def on_device(state, coupling, coupling_t, factor, cofactor, rates):
        slots = 2 * rows // cols
        width = slots * BS
        any_space = pl.BlockSpec(memory_space=pl.ANY)
        vmem = pl.BlockSpec(memory_space=pltpu.VMEM)
        f32, bf16 = jnp.float32, jnp.bfloat16
        dma = pltpu.SemaphoreType.DMA
        return pl.pallas_call(
            functools.partial(kernel, rows, cols, slots),
            out_shape=jax.ShapeDtypeStruct((BS, 1, width), f32),
            in_specs=[any_space] * 6,
            out_specs=vmem,
            scratch_shapes=[
                pltpu.VMEM((BS, 1, width), f32),
                pltpu.VMEM((slots, BS, BS), f32),
                pltpu.VMEM((slots, BS, BS), bf16),
                pltpu.VMEM((slots, BS, BS), bf16),
                pltpu.VMEM((slots, BS, BS), bf16),
                pltpu.VMEM((slots, BS, BS), bf16),
                pltpu.VMEM((STEPS, 2, 2, BS, BS), f32),
                pltpu.VMEM((slots, 1, BS), f32),
                pltpu.VMEM((slots, 8, BS), f32),
                pltpu.VMEM((STEPS, 8, BS), f32),
                pltpu.VMEM((STEPS, 2, BS, BS), bf16),
                pltpu.VMEM((STEPS, slots, 2, BS, BS), bf16),
                dma((2 + slots,)),
                dma((STEPS, 2, 2, 2)),
                dma((STEPS, 2)),
                dma((STEPS,)),
                dma((STEPS,)),
                dma((slots,)),
                dma((slots,)),
                dma((slots,)),
                dma((slots,)),
                dma((slots,)),
                dma((slots,)),
                dma((STEPS, 8)),
                dma((STEPS,)),
                dma((STEPS, slots, rows // XS - 1 + XS - 1)),
                dma((STEPS, slots, XS)),
                dma((STEPS, 3 + XS)),
                dma((XS + 1,)),
            ],
            compiler_params=pltpu.CompilerParams(
                collective_id=0, has_side_effects=True, vmem_limit_bytes=63000 * 1024
            ),
        )(
            state,
            coupling.reshape(BS, width),
            coupling_t.reshape(2, BS, width),
            factor.reshape(slots, 8, BS),
            cofactor.reshape(slots, 8, BS),
            rates,
        )

    return jax.shard_map(
        on_device,
        mesh=mesh,
        in_specs=(
            P("row", "col", None),
            P("row", "col", None),
            P(None, "row", "col", None),
            P(None, "col", "row", None),
            P(None, "col", "row", None),
            P(None, "col", None),
        ),
        out_specs=P("row", "col", None),
        check_vma=False,
    )
```

time: 162 us -> 93.9 us (0.58)
  the two profiles are of different devices: /device:TPU:67 before, /device:TPU:135 now
where the time goes in v2:
time: 93.9 us; the launch traced here: 93.8 us
  Pallas kernels  90.8 us (97%)
  local copies, waits for them, and re-layouts  2.91 us (3%)
    pallas_call x1, Pallas kernels, on_device(): pl.pallas_call(functools.partial(kernel, rows, cols, slots), out_shape=ja...  90.8 us
    unnamed x1, local copies, waits for them, and re-layouts  2.91 us

profile of v2, /device:TPU:135, one launch (start us, length us, event | category | flops | bytes accessed | tf_op | source)
XLA Modules:
  0.0 93.8 jit_solution(16433700705221883829)
XLA Ops:
  0.0 90.8 %shard_map.64 = f32[256,1,1024]{2,1,0:T(1,128)} custom-call(f32[256,1,1024]{2,1,0:T(1,128)} %st_in.1, bf16[256,1024]{1,0:T(8,128)(2,1)} %bitcast.5, bf16[2,256,1024]{2,1,0:T(8,128)(2,1)} %bitcast.4, f32[4,8,256]{2,1,0:T(8,128)} %bitcast.6, f32[4,8,256]{2,1,0:T(8,128)} %bitcast.7, f32[4,1,256]{2,1,0:T(1,128)} %e_in.1), custom_call_target="tpu_custom_call" | custom-call | tf_op jit(solution)/shard_map/pallas_call | solution.py:421
  90.8 2.9 %copy.8 = f32[256,1,1024]{2,1,0:T(1,128)} copy(f32[256,1,1024]{2,1,0:T(1,128)} %shard_map.64) | data formatting | bytes 2097152

commit v3 on v2

--- a/solution.py
+++ b/solution.py
@@ -18,6 +18,30 @@
     return hi, (a - hi.astype(jnp.float32)).astype(jnp.bfloat16)
 
 
+QROWS = BS // XS
+TOP = 32768.0
+
+
+def bound(a):
+    largest = jnp.max(jnp.max(jnp.abs(a), axis=0, keepdims=True), axis=1, keepdims=True)
+    return (jnp.maximum(largest, 1e-30) * 1.01).astype(jnp.bfloat16).astype(jnp.float32)
+
+
+def encode(a, top):
+    v = a * (TOP / top)
+    p = v * v
+    p = p * p
+    p = p * p
+    return jnp.where(v < 0, -p, p).astype(jnp.bfloat16)
+
+
+def decode(code, top):
+    u = code.astype(jnp.float32)
+    fourth = lax.rsqrt(lax.rsqrt(jnp.maximum(jnp.abs(u), 1.2e-38)))
+    v = fourth * lax.rsqrt(fourth) * (top / TOP)
+    return jnp.where(u < 0, -v, jnp.where(u > 0, v, 0.0))
+
+
 def nn(a, b):
     return lax.dot_general(a, b, (((1,), (0,)), ((), ())), preferred_element_type=jnp.float32)
 
@@ -35,10 +59,10 @@
 def kernel(
     rows, cols, slots,
     st_in, cp_in, ct_in, p_in, q_in, e_in, out,
-    st, w, a0, a1, at0, at1, pq, ev, es, el, xr, zs,
+    st, w, a0, a1, at0, at1, pq, own_pq, ev, es, el, xr, zs, xd, zd,
     loc_sem, pq_ssem, pq_rsem, e_ssem, e_rsem,
     at_ssem, at0_rsem, atf_ssem, at1_rsem, a1_ssem, a1_rsem,
-    xr_ssem, xr_rsem, z_ssem, z_rsem, sv_ssem, er_ssem,
+    xr_ssem, xr_rsem, z_ssem, z_rsem, sv_ssem, er_ssem, fw_ssem, go_sem,
 ):
     r, c = lax.axis_index("row"), lax.axis_index("col")
     y, x = r // XS, lax.rem(r, XS)
@@ -90,6 +114,15 @@
 
         expected = expected + jnp.where(is_s[s], XS, 0) - jnp.where(is_s[s] & (c == tcol), 1, 0)
 
+        if s == 1:
+
+            @pl.when(is_s[1] & (c != tcol))
+            def _():
+                greet(r, tcol)
+
+            expected = expected + jnp.where((c == tcol) & (c != sc[1]), 1, 0)
+            continue
+
         @pl.when(is_s[s])
         def _():
             for k in range(1, rows):
@@ -114,28 +147,31 @@
         cp.start()
     ld_e = pltpu.make_async_copy(e_in, ev, loc_sem.at[1 + slots])
     ld_e.start()
+    ld_pq = [
+        pltpu.make_async_copy(ref, own_pq.at[:, t], loc_sem.at[2 + slots + t])
+        for t, ref in enumerate((p_in, q_in))
+    ]
+    for cp in ld_pq:
+        cp.start()
     ld_e.wait()
+    for cp in ld_pq:
+        cp.wait()
     es[...] = jnp.broadcast_to(ev[...], es.shape)
     with jax.named_scope("barrier"):
         pl.semaphore_wait(barrier, expected)
 
-    def to_solver(s, side, q):
+    def to_solver(side, q):
+        slot = q + 2 * side
+        m = c + cols * slot
         if side == 0:
-            m = c + cols * q
-            slot = q
-            dr, dc = m, lax.rem(nb - 1 - s - m, cols)
+            dr, dc = m, lax.rem(nb - 1 - m, cols)
         else:
-            m = c + cols * (2 + q)
-            if s == 1:
-                m = m - jnp.where(c == cols - 1, cols, 0)
-            slot = m // cols
-            dr, dc = nb - 1 - s - m, c
+            dr, dc = nb - 1 - m, c
         mine = (dr == r) & (dc == c)
-        for t, ref in enumerate((p_in, q_in)):
-            src = ref.at[slot]
-            dst = pq.at[s, side, t, pl.ds(pl.multiple_of(r * 8, 8), 8), :]
-            send(~mine, src, dst, pq_ssem.at[s, side, q, t], pq_rsem.at[s, side], (dr, dc))
-            pl.when(mine)(pltpu.make_async_copy(src, dst, pq_rsem.at[s, side]).start)
+        src = own_pq.at[slot]
+        dst = pq.at[0, side, :, pl.ds(pl.multiple_of(r * 8, 8), 8), :]
+        send(~mine, src, dst, pq_ssem.at[side, q], pq_rsem.at[0, side], (dr, dc))
+        pl.when(mine)(pltpu.make_async_copy(src, dst, pq_rsem.at[0, side]).start)
 
     def rate_to_solver(s):
         have = c == tcol
@@ -143,35 +179,48 @@
         send(have & ~mine, es.at[tslot], el.at[s], e_ssem.at[s], e_rsem.at[s], (r, sc[s]))
         pl.when(have & mine)(pltpu.make_async_copy(es.at[tslot], el.at[s], e_rsem.at[s]).start)
 
+    for side in range(2):
+        for q in range(2):
+            to_solver(side, q)
     for s in range(STEPS):
-        for side in range(2):
-            for q in range(2):
-                to_solver(s, side, q)
         rate_to_solver(s)
-
-    for pred, cp in pending:
-        pl.when(pred)(cp.wait_send)
-    pending.clear()
 
     def at_needed(g, u):
         m = c + cols * u
         return (m >= g - 1) & (m <= nb - 2 - g)
 
     g = lax.rem(r + rows // 2, rows)
-    for u in reversed(range(slots)):
-        send(at_needed(g, u), ct_in.at[0, :, pl.ds(u * BS, BS)], at0.at[u],
-             at_ssem.at[u], at0_rsem.at[u], (g, c))
-
     c_dn = lax.rem(c + cols - 1, cols)
+    urgent = nb - 2 - g
 
     def step1_target(row, m):
         return (row <= m) & (row + m < nb - 2)
 
-    for u in range(slots):
-        wrap = jnp.where(c == 0, 1, 0)
-        du = u - wrap
-        send((du >= 0) & step1_target(r, c_dn + cols * du), cp_in.at[:, pl.ds(u * BS, BS)],
-             a1.at[jnp.maximum(du, 0)], a1_ssem.at[u], a1_rsem.at[jnp.maximum(du, 0)], (r, c_dn))
+    def at_send(u, first):
+        at_once = c + cols * u == urgent
+        send(at_needed(g, u) & (at_once if first else ~at_once), ct_in.at[0, :, pl.ds(u * BS, BS)],
+             at0.at[u], at_ssem.at[u], at0_rsem.at[u], (g, c))
+
+    def bulk_sends():
+        for u in reversed(range(slots)):
+            at_send(u, False)
+        for u in range(slots):
+            wrap = jnp.where(c == 0, 1, 0)
+            du = u - wrap
+            send((du >= 0) & step1_target(r, c_dn + cols * du), cp_in.at[:, pl.ds(u * BS, BS)],
+                 a1.at[jnp.maximum(du, 0)], a1_ssem.at[u], a1_rsem.at[jnp.maximum(du, 0)], (r, c_dn))
+
+    with jax.named_scope("pq_sent"):
+        for pred, cp in pending:
+            pl.when(pred)(cp.wait_send)
+        pending.clear()
+        for dy in range(1, ys):
+            pl.semaphore_signal(
+                go_sem, inc=1, device_id=(lax.rem(r + dy * XS, rows), c), device_id_type=MESH
+            )
+
+    for u in range(1, slots):
+        at_send(u, True)
 
     with jax.named_scope("local_in"):
         ld_st.wait()
@@ -187,7 +236,20 @@
         return d, m, j, m <= d
 
     def quarter(ref, q):
-        return ref.at[:, pl.ds(pl.multiple_of(q * (BS // XS), BS // XS), BS // XS), :]
+        return ref.at[q]
+
+    def write_code(ref, a, top):
+        code = encode(a, top)
+        for q in range(XS):
+            ref[q, :QROWS] = code[q * QROWS:(q + 1) * QROWS]
+            ref[q, QROWS:] = jnp.broadcast_to(top, (8, BS)).astype(jnp.bfloat16)
+
+    def read_code(ref, dst, order):
+        for q in order:
+            top = ref[q, QROWS:QROWS + 1, :].astype(jnp.float32)
+            hi, lo = split2(decode(ref[q, :QROWS], top))
+            dst[0, q * QROWS:(q + 1) * QROWS] = hi
+            dst[1, q * QROWS:(q + 1) * QROWS] = lo
 
     def place(s, u):
         d = nb - 1 - s
@@ -283,53 +345,58 @@
         send(member & ~to_early, xr.at[s], xr.at[s], xr_ssem.at[s, 7], xr_rsem.at[s], (r, mate))
 
     def solve(s):
-        for side in range(2):
-            with jax.named_scope(f"wait_pq{s}{side}"):
-                pltpu.make_async_copy(pq.at[s, side], pq.at[s, side], pq_rsem.at[s, side]).wait()
-        pltpu.make_async_copy(el.at[s], el.at[s], e_rsem.at[s]).wait()
+        right = jnp.where(r == rows - 1, 0, 1) if s == 1 else 1
         left_e = jnp.transpose(el[s])[:, :1]
         right_e = ev[us[s]]
         mid = dot3(nn, pq[s, 0, 1], w[us[s]])
-        mid = dot3(nt, mid, pq[s, 1, 1])
+        mid = dot3(nt, mid, pq[s, right, 1])
         mid = mid / (left_e + right_e)
         mid = dot3(nn, pq[s, 0, 0], mid)
-        sol = -dot3(nt, mid, pq[s, 1, 0])
-        hi, lo = split2(sol)
-        xr[s, 0] = hi
-        xr[s, 1] = lo
+        sol = -dot3(nt, mid, pq[s, right, 0])
+        top = bound(sol)
+        write_code(xr.at[s], sol, top)
         if s == 0:
-            zs[s, us[s], 0] = hi
-            zs[s, us[s], 1] = lo
+            write_code(zs.at[s, us[s]], sol, top)
         else:
             last = r == rows - 1
 
             @pl.when(last)
             def _():
-                th, tl = split2(jnp.transpose(sol))
-                zs[s, us[s], 0] = th
-                zs[s, us[s], 1] = tl
+                write_code(zs.at[s, us[s]], jnp.transpose(sol), top)
 
             @pl.when(~last)
             def _():
-                zs[s, us[s], 0] = hi
-                zs[s, us[s], 1] = lo
+                write_code(zs.at[s, us[s]], sol, top)
 
             @pl.when(~last & (c == tcol))
             def _():
-                zs[s, tslot, 0] = hi
-                zs[s, tslot, 1] = lo
+                write_code(zs.at[s, tslot], sol, top)
         w[us[s]] = sol
 
-    def terms(z, s, a, at, dot):
-        return dot(a, z[0]) + dot(a, z[1]) + nn(xr[s, 0], at) + nn(xr[s, 1], at)
+    def terms(z, a, at, dot):
+        return dot(a, z[0]) + dot(a, z[1]) + nn(xd[0], at) + nn(xd[1], at)
 
     u1 = us[1]
+    def operators_ready(s):
+        for side in range(2):
+            on = is_s[s] & (r < rows - 1) if (s, side) == (1, 1) else is_s[s]
+            arrived(on, pq.at[s, side], pq_rsem.at[s, side])
+            if s == 0:
+                to, dev = (on, (r, sc[1])) if side == 0 else (on & (r >= 1), (jnp.maximum(r - 1, 0), c))
+                send(to, pq.at[0, side], pq.at[1, side], fw_ssem.at[side], pq_rsem.at[1, side], dev)
+        arrived(is_s[s], el.at[s], e_rsem.at[s])
+
+    with jax.named_scope("wait_pq00"):
+        operators_ready(0)
     with jax.named_scope("solve0"):
         pl.when(is_s[0])(functools.partial(solve, 0))
     early_sends()
     solver_sends(0)
     relay(0, us[0], is_s[0])
     row_sends(0)
+    with jax.named_scope("wait_go"):
+        pl.semaphore_wait(go_sem, ys - 1)
+    bulk_sends()
 
     with jax.named_scope("early_wait_xr"):
         arrived(is_s[1], xr.at[0], xr_rsem.at[0])
@@ -341,14 +408,21 @@
     with jax.named_scope("early_wait_at"):
         arrived(is_s[1], at0.at[u1], at0_rsem.at[u1])
 
+    @pl.when(is_s[1])
+    def _():
+        read_code(xr.at[0], xd, range(XS))
+
     @pl.when(is_s[1] & (r == rows - 1))
     def _():
-        w[u1] = w[u1] - terms(xr.at[0], 0, a0[u1], at0[u1], nt)
+        w[u1] = w[u1] - terms(xd, a0[u1], at0[u1], nt)
 
     @pl.when(early_on)
     def _():
-        w[u1] = w[u1] - terms(zs.at[0, u1], 0, a0[u1], at0[u1], nn)
-
+        read_code(zs.at[0, u1], zd, range(XS))
+        w[u1] = w[u1] - terms(zd, a0[u1], at0[u1], nn)
+
+    with jax.named_scope("wait_pq1"):
+        operators_ready(1)
     with jax.named_scope("solve1"):
         pl.when(is_s[1])(functools.partial(solve, 1))
     solver_sends(1)
@@ -356,48 +430,55 @@
     relay(1, tslot, is_s[1] & (c == tcol) & (r < rows - 1))
     row_sends(1)
 
+    def update(s, a_ref, at_ref):
+        last_m = nb - 2 - s - r
+
+        @pl.when(r <= last_m)
+        def _():
+            read_code(xr.at[s], xd, range(XS))
+
+        for u in range(slots):
+            m = c + cols * u
+            target = (r <= m) & (m <= last_m)
+            if s == 0:
+                target = target & ~(is_s[1] & (u == u1))
+
+            @pl.when(target)
+            def _(u=u):
+                read_code(zs.at[s, u], zd, range(XS))
+                w[u] = w[u] - terms(zd, a_ref[u], at_ref[u], nt if u < 2 else nn)
+
+    with jax.named_scope("relay0a"):
+        relays(0, True)
+    with jax.named_scope("relay1a"):
+        relays(1, True)
+    with jax.named_scope("relay0b"):
+        relays(0, False)
     with jax.named_scope("at_forward"):
         for u in reversed(range(slots)):
             arrived(at_needed(r, u) & ~(is_s[1] & (u == u1)), at0.at[u], at0_rsem.at[u])
             send(at_needed(r, u) & (r >= 1), at0.at[u], at1.at[u], atf_ssem.at[u], at1_rsem.at[u],
                  (jnp.maximum(r - 1, 0), c))
 
-    def update(s, a_ref, at_ref):
-        for u in range(slots):
-            m = c + cols * u
-            target = (r <= m) & (r + m < nb - 1 - s)
-            if s == 0:
-                target = target & ~(is_s[1] & (u == u1))
-
-            @pl.when(target)
-            def _(u=u):
-                w[u] = w[u] - terms(zs.at[s, u], s, a_ref[u], at_ref[u], nt if u < 2 else nn)
-
-    with jax.named_scope("relay0a"):
-        relays(0, True)
-    with jax.named_scope("relay0b"):
-        relays(0, False)
+    with jax.named_scope("relay1b"):
+        relays(1, False)
     with jax.named_scope("row0"):
         row_relay(0)
-    with jax.named_scope("relay1a"):
-        relays(1, True)
+    with jax.named_scope("row1"):
+        row_relay(1)
     with jax.named_scope("rest0"):
         for u in range(slots):
             rest(0, u)
     with jax.named_scope("update0"):
         update(0, a0, at0)
-    with jax.named_scope("relay1b"):
-        relays(1, False)
-    with jax.named_scope("row1"):
-        row_relay(1)
-    with jax.named_scope("rest1"):
-        for u in range(slots):
-            rest(1, u)
     with jax.named_scope("wait_a1_at1"):
         for u in range(slots):
             need = step1_target(r, c + cols * u)
             arrived(need, a1.at[u], a1_rsem.at[u])
             arrived(at_needed(r + 1, u) & (r < rows - 1), at1.at[u], at1_rsem.at[u])
+    with jax.named_scope("rest1"):
+        for u in range(slots):
+            rest(1, u)
     with jax.named_scope("update1"):
         update(1, a1, at1)
     with jax.named_scope("write_out"):
@@ -431,13 +512,16 @@
                 pltpu.VMEM((slots, BS, BS), bf16),
                 pltpu.VMEM((slots, BS, BS), bf16),
                 pltpu.VMEM((STEPS, 2, 2, BS, BS), f32),
+                pltpu.VMEM((slots, 2, 8, BS), f32),
                 pltpu.VMEM((slots, 1, BS), f32),
                 pltpu.VMEM((slots, 8, BS), f32),
                 pltpu.VMEM((STEPS, 8, BS), f32),
-                pltpu.VMEM((STEPS, 2, BS, BS), bf16),
-                pltpu.VMEM((STEPS, slots, 2, BS, BS), bf16),
-                dma((2 + slots,)),
-                dma((STEPS, 2, 2, 2)),
+                pltpu.VMEM((STEPS, XS, QROWS + 8, BS), bf16),
+                pltpu.VMEM((STEPS, slots, XS, QROWS + 8, BS), bf16),
+                pltpu.VMEM((2, BS, BS), bf16),
+                pltpu.VMEM((2, BS, BS), bf16),
+                dma((4 + slots,)),
+                dma((2, 2)),
                 dma((STEPS, 2)),
                 dma((STEPS,)),
                 dma((STEPS,)),
@@ -453,6 +537,8 @@
                 dma((STEPS, slots, XS)),
                 dma((STEPS, 3 + XS)),
                 dma((XS + 1,)),
+                dma((2,)),
+                pltpu.SemaphoreType.REGULAR,
             ],
             compiler_params=pltpu.CompilerParams(
                 collective_id=0, has_side_effects=True, vmem_limit_bytes=63000 * 1024

time: 93.9 us -> 77.6 us (0.83)
  the two profiles are of different devices: /device:TPU:135 before, /device:TPU:1 now
where the time goes in v3:
time: 77.6 us; the launch traced here: 77.3 us
  Pallas kernels  74.4 us (96%)
  local copies, waits for them, and re-layouts  2.91 us (4%)
    pallas_call x1, Pallas kernels, on_device(): pl.pallas_call(functools.partial(kernel, rows, cols, slots), out_shape=ja...  74.4 us
    unnamed x1, local copies, waits for them, and re-layouts  2.91 us

profile of v3, /device:TPU:1, one launch (start us, length us, event | category | flops | bytes accessed | tf_op | source)
XLA Modules:
  0.0 77.3 jit_solution(16218976494769190952)
XLA Ops:
  0.0 74.4 %shard_map.64 = f32[256,1,1024]{2,1,0:T(1,128)} custom-call(f32[256,1,1024]{2,1,0:T(1,128)} %st_in.1, bf16[256,1024]{1,0:T(8,128)(2,1)} %bitcast.5, bf16[2,256,1024]{2,1,0:T(8,128)(2,1)} %bitcast.4, f32[4,8,256]{2,1,0:T(8,128)} %bitcast.6, f32[4,8,256]{2,1,0:T(8,128)} %bitcast.7, f32[4,1,256]{2,1,0:T(1,128)} %e_in.1), custom_call_target="tpu_custom_call" | custom-call | tf_op jit(solution)/shard_map/pallas_call | solution.py:502
  74.4 2.9 %copy.8 = f32[256,1,1024]{2,1,0:T(1,128)} copy(f32[256,1,1024]{2,1,0:T(1,128)} %shard_map.64) | data formatting | bytes 2097152
